TPU v7x, 8 devices: a whole 2x2x1 slice. The times are simulated.
8 devices in a mesh: exam: 2 (over z, y), rows: 4 (over x, core).
Axes of the slice: x: 2, y: 2, z: 1, core: 2. Of those that a mesh axis runs over, the one named last changes fastest.
Arguments:
- kspace: float32 [2, 8, 8192], P(None, None, ('exam', 'rows')), parts along dimension 2
- weight_row: float32 [6, 8192], P(None, ('exam', 'rows')), parts along dimension 1
- weight_col: float32 [6, 8192], P(None, ('exam', 'rows')), parts along dimension 1
- row_idx: int32 [8192], P(('exam', 'rows')), parts along dimension 0
- col_idx: int32 [8192], P(('exam', 'rows')), parts along dimension 0
- counts: int32 [8], P(('exam', 'rows')), parts along dimension 0
- coil_maps: float32 [2, 8, 384, 768], P(None, None, None, ('exam', 'rows')), parts along dimension 3
- deapod: float32 [384], replicated
Outputs:
- output: float32 [2, 768, 384], P(None, ('exam', 'rows')), parts along dimension 1
There are 2 independent parts. A program takes and returns all parts, laid end to end along the dimension named above; an argument that names none is the same for every part.
All inputs are finite; a program needn't handle non-finite values.
Results may differ from a plain program's by a relative error of at most 0.001.
Values are sent between devices in bfloat16 or wider.
A program may use at most 1 GiB of HBM per device.

v0:
```python
import functools
import math

import jax
import jax.numpy as jnp
import numpy as np
from jax import lax
from jax.experimental import pallas as pl
from jax.experimental.pallas import tpu as pltpu
from jax.sharding import PartitionSpec as P

MESH = pl.DeviceIdType.MESH
F32 = jnp.float32
BF16 = jnp.bfloat16
LANES = 128
SUB = 8


def dft_tables(img_size, row_devs):
    grid_size = 2 * img_size
    frequency = np.arange(grid_size)[None, :] - img_size
    pixel_pos = np.arange(img_size)[:, None] - img_size // 2
    angle = ((frequency * pixel_pos) % grid_size).astype(np.float64) * (2.0 * math.pi / grid_size)
    table = np.stack([np.cos(angle), np.sin(angle)]).astype(np.float32).astype(jnp.bfloat16)
    block = grid_size // row_devs
    order = np.concatenate([np.arange(SUB, block - SUB), np.arange(SUB), np.arange(block - SUB, block)])
    by_core = []
    for core in range(2):
        rows = np.concatenate([(2 * chip + core) * block + order for chip in range(row_devs // 2)])
        by_core.append(table[:, :, rows])
    return table, np.stack(by_core)


def grid_kernel(data_ref, tab_hbm, h_ref, edge_ref, acc_a, acc_b, lvec, addr_v, gbuf, tab_v, addr_s, tab_sem, addr_sem, *, pitch, cols):
    chip = lax.axis_index('rows') // 2
    groups = acc_a.shape[0] // pitch
    half = tab_v.shape[1] // 2
    tab_copy = pltpu.make_async_copy(tab_hbm.at[:, pl.ds(pl.multiple_of(chip * 2 * half, 2 * half), 2 * half), :], tab_v, tab_sem)
    tab_copy.start()
    addr_v[...] = data_ref[24:32, :].astype(jnp.int32)
    addr_copy = pltpu.make_async_copy(addr_v, addr_s, addr_sem)
    addr_copy.start()

    @pl.loop(0, groups)
    def _(g):
        base = pl.multiple_of(g * pitch, SUB)
        acc_a[pl.ds(base, pitch), :] = jnp.zeros((pitch, LANES), F32)
        acc_b[pl.ds(base, pitch), :] = jnp.zeros((pitch, LANES), F32)

    addr_copy.wait()
    count = addr_s[7, 0]
    slot = lax.broadcasted_iota(jnp.int32, (2 * SUB, LANES), 0).astype(F32)
    tap_row = lax.broadcasted_iota(jnp.int32, (SUB, LANES), 0)

    @pl.loop(0, (count + LANES - 1) // LANES)
    def _(blk):
        first = pl.multiple_of(blk * LANES, LANES)
        wr8 = data_ref[16:24, pl.ds(first, LANES)]
        tap = slot - wr8[6:7, :]
        wrs = jnp.where(tap == 0.0, wr8[0:1, :], 0.0)
        for a in range(1, 6):
            wrs = wrs + jnp.where(tap == float(a), wr8[a:a + 1, :], 0.0)
        y16 = data_ref[0:16, pl.ds(first, LANES)]
        for part in range(2):
            w_part = wrs[part * SUB:(part + 1) * SUB, :]
            full = jnp.concatenate([y16[ch:ch + 1, :] * w_part for ch in range(16)], axis=0)
            lvec[:, part * LANES:(part + 1) * LANES] = full.T
        wc8 = jnp.where(tap_row < 6, data_ref[24:32, pl.ds(first, LANES)], 0.0)

        def contribution(k):
            wide = jnp.broadcast_to(wc8[:, k:k + 1], (SUB, LANES))
            lo = jnp.broadcast_to(lvec[k:k + 1, 0:LANES], (SUB, LANES))
            hi = jnp.broadcast_to(lvec[k:k + 1, LANES:2 * LANES], (SUB, LANES))
            return wide * lo, wide * hi

        for k in range(0, LANES, 2):
            at_a = addr_s[6, first + k]
            at_b = addr_s[6, first + k + 1]
            a_lo, a_hi = contribution(k)
            b_lo, b_hi = contribution(k + 1)
            old_a_lo = acc_a[pl.ds(at_a, SUB), :]
            old_a_hi = acc_a[pl.ds(at_a + pitch, SUB), :]
            old_b_lo = acc_b[pl.ds(at_b, SUB), :]
            old_b_hi = acc_b[pl.ds(at_b + pitch, SUB), :]
            acc_a[pl.ds(at_a, SUB), :] = old_a_lo + a_lo
            acc_a[pl.ds(at_a + pitch, SUB), :] = old_a_hi + a_hi
            acc_b[pl.ds(at_b, SUB), :] = old_b_lo + b_lo
            acc_b[pl.ds(at_b + pitch, SUB), :] = old_b_hi + b_hi

    def rows_sum(g, start, size):
        at = pl.multiple_of(g * pitch + start, SUB)
        total = acc_a[pl.ds(at, size), :] + acc_b[pl.ds(at, size), :]
        if start == 0:
            wrap = pl.multiple_of(g * pitch + cols, SUB)
            head = total[0:SUB] + (acc_a[pl.ds(wrap, SUB), :] + acc_b[pl.ds(wrap, SUB), :])
            total = jnp.concatenate([head, total[SUB:]], axis=0)
        return total

    chunk = 128
    for start in range(0, cols, chunk):
        edge_ref[0, start:start + chunk, :] = rows_sum(1, start, chunk)
        edge_ref[1, start:start + chunk, :] = rows_sum(groups - 2, start, chunk)
        edge_ref[2, start:start + chunk, :] = rows_sum(0, start, chunk) + rows_sum(groups - 1, start, chunk)
    tab_copy.wait()

    @pl.loop(0, (groups - 4) // 2)
    def _(pair):
        for start in range(0, cols, chunk):
            for side in range(2):
                gbuf[start:start + chunk, side * LANES:(side + 1) * LANES] = rows_sum(2 + 2 * pair + side, start, chunk).astype(BF16)
        column_pass(tab_v, gbuf, h_ref, pair)


def column_pass(tab_v, gbuf, h_ref, pair):
    size = tab_v.shape[1]
    half = size // 2
    lane = lax.broadcasted_iota(jnp.int32, (half, LANES), 1)
    sign = jnp.where(lane < LANES // 2, -1.0, 1.0).astype(F32)
    grid = gbuf[...]
    by_cos = jnp.dot(tab_v[0], grid, preferred_element_type=F32)
    by_sin = jnp.dot(tab_v[1], grid, preferred_element_type=F32)
    for j_half in range(2):
        turned = []
        for side in range(2):
            part = (slice(j_half * half, (j_half + 1) * half), slice(side * LANES, (side + 1) * LANES))
            mixed = by_cos[part] + sign * pltpu.roll(by_sin[part], LANES // 2, 1)
            mixed = jnp.concatenate([mixed, jnp.zeros((LANES - half, LANES), F32)], axis=0)
            turned.append(mixed.T)
        for ch in range(16):
            rows = slice(ch * SUB, (ch + 1) * SUB)
            tile = jnp.concatenate([turned[0][rows], turned[1][rows]], axis=0).astype(BF16)
            if pair is None:
                h_ref[j_half, ch] = tile
            else:
                h_ref[j_half, ch, pl.ds(pl.multiple_of(pair * 16, 16), 16), :] = tile


def image_kernel(h_own, h_oth, e_own, e_oth, tab_hbm, tab2_hbm, maps_hbm, dcol_ref, drow_ref, out_ref,
                 e_v, margins, gbuf, e_turn, tab_v, tab2_v, maps_v, h_all, img, pieces,
                 load_sem, h_load_sem, m_send, m_recv, h_send, h_recv, t_send, t_recv, p_send, p_recv):
    me = lax.axis_index('rows')
    chip = me // 2
    core = me % 2
    peers = [2 * chip + 1 - core, 2 * (1 - chip) + core, 2 * (1 - chip) + 1 - core]
    partner = {'rows': peers[0]}
    block = h_all.shape[2] // 2
    inner = h_own.shape[2]
    half = img.shape[2]

    tab_copy = pltpu.make_async_copy(tab_hbm.at[:, pl.ds(pl.multiple_of(chip * 2 * half, 2 * half), 2 * half), :], tab_v, load_sem.at[0])
    tab2_copy = pltpu.make_async_copy(tab2_hbm, tab2_v, load_sem.at[1])
    maps_copy = pltpu.make_async_copy(maps_hbm, maps_v, load_sem.at[2])
    e_copies = [pltpu.make_async_copy(e.at[0:2], e_v.at[s], load_sem.at[3 + s]) for s, e in enumerate((e_own, e_oth))]
    places = [pl.multiple_of(chip * block, 16), pl.multiple_of((1 - chip) * block, 16)]
    h_copies = [pltpu.make_async_copy(h.at[core], h_all.at[core, :, pl.ds(places[s], inner), :], h_load_sem.at[s]) for s, h in enumerate((h_own, h_oth))]
    for copy in e_copies + [tab_copy] + h_copies + [tab2_copy, maps_copy]:
        copy.start()

    barrier = pltpu.get_barrier_semaphore()
    for peer in peers:
        pl.semaphore_signal(barrier, inc=1, device_id={'rows': peer}, device_id_type=MESH)
    pl.semaphore_wait(barrier, 3)

    m_copies = [pltpu.make_async_remote_copy(src_ref=e.at[2], dst_ref=margins.at[s], send_sem=m_send.at[s], recv_sem=m_recv.at[s], device_id=partner, device_id_type=MESH) for s, e in enumerate((e_own, e_oth))]
    for copy in m_copies:
        copy.start()
    h_sends = [pltpu.make_async_remote_copy(src_ref=h.at[1 - core], dst_ref=h_all.at[core, :, pl.ds(places[s], inner), :], send_sem=h_send.at[s], recv_sem=h_recv.at[s], device_id=partner, device_id_type=MESH) for s, h in enumerate((h_own, h_oth))]
    for copy in h_sends:
        copy.start()

    low = lax.broadcasted_iota(jnp.int32, (128, LANES), 1) % SUB < SUB // 2
    for copy in e_copies + [tab_copy]:
        copy.wait()
    for copy in m_copies:
        copy.wait()
    t_sends = []
    for s in range(2):
        from_low = lax.rem(s + 1 - core, 2)
        from_high = lax.rem(s + core, 2)
        for start in range(0, gbuf.shape[0], 128):
            rows = slice(start, start + 128)
            gbuf[rows, 0:LANES] = (e_v[s, 0, rows, :] + jnp.where(low, margins[from_low, rows, :], 0.0)).astype(BF16)
            gbuf[rows, LANES:2 * LANES] = (e_v[s, 1, rows, :] + jnp.where(low, 0.0, margins[from_high, rows, :])).astype(BF16)
        column_pass(tab_v, gbuf, e_turn.at[s], None)
        edge_place = pl.ds(pl.multiple_of(places[s] + inner, 16), 2 * SUB)
        h_all[core, :, edge_place, :] = e_turn[s, core]
        send = pltpu.make_async_remote_copy(src_ref=e_turn.at[s, 1 - core], dst_ref=h_all.at[core, :, edge_place, :], send_sem=t_send.at[s], recv_sem=t_recv.at[s], device_id=partner, device_id_type=MESH)
        send.start()
        t_sends.append(send)

    rows_half = 2 * half

    def row_pass(parity, i_half, fresh):
        place = pl.ds(pl.multiple_of(i_half * rows_half, rows_half), rows_half)

        @pl.loop(0, 8)
        def _(coil):
            field = jnp.concatenate([h_all[parity, coil], h_all[parity, coil + 8]], axis=1)
            by_cos = jnp.dot(tab2_v[parity, 0, place, :], field, preferred_element_type=F32)
            by_sin = jnp.dot(tab2_v[parity, 1, place, :], field, preferred_element_type=F32)
            img_re = (by_cos[:, :LANES] - by_sin[:, LANES:])[:, :half]
            img_im = (by_sin[:, :LANES] + by_cos[:, LANES:])[:, :half]
            map_re = maps_v[0, coil, place, :]
            map_im = maps_v[1, coil, place, :]
            add_re = map_re * img_re + map_im * img_im
            add_im = map_re * img_im - map_im * img_re
            if fresh:
                first = coil == 0
                img[0, place, :] = jnp.where(first, 0.0, img[0, place, :]) + add_re
                img[1, place, :] = jnp.where(first, 0.0, img[1, place, :]) + add_im
            else:
                img[0, place, :] += add_re
                img[1, place, :] += add_im

    for copy in h_copies + [tab2_copy, maps_copy]:
        copy.wait()
    img[...] = jnp.zeros_like(img)
    row_pass(core, 1 - chip, False)
    row_pass(core, chip, False)
    for copy in h_sends + t_sends:
        copy.wait()
    p_copies = []

    def send_piece(rel):
        target = peers[rel - 1]
        copy = pltpu.make_async_remote_copy(src_ref=img.at[:, pl.ds(pl.multiple_of(target * half, SUB), half), :], dst_ref=pieces.at[rel], send_sem=p_send.at[rel - 1], recv_sem=p_recv.at[rel - 1], device_id={'rows': target}, device_id_type=MESH)
        copy.start()
        p_copies.append(copy)

    row_pass(1 - core, 1 - chip, False)
    send_piece(2)
    send_piece(3)
    row_pass(1 - core, chip, False)
    send_piece(1)
    pieces[0] = img[:, pl.ds(pl.multiple_of(me * half, SUB), half), :]
    for copy in p_copies:
        copy.wait()
    scale = dcol_ref[pl.ds(pl.multiple_of(me * half, SUB), half), :] * drow_ref[...]
    for q in range(2):
        row = []
        for src in range(4):
            rel = lax.rem(src // 2 + chip, 2) * 2 + lax.rem(src % 2 + core, 2)
            row.append(pieces[rel, q])
        out_ref[q] = jnp.concatenate(row, axis=1) * scale


def solution(mesh):
    row_devs = mesh.shape['rows']
    part_axes = ('exam', 'rows')

    def local_step(kspace, weight_row, weight_col, row_idx, col_idx, counts, coil_maps, deapod):
        img_size = deapod.shape[0]
        cols = 2 * img_size
        block_rows = cols // row_devs
        samples = kspace.shape[2]
        pitch = cols + SUB
        half = img_size // row_devs
        groups = block_rows // SUB + 2
        me = lax.axis_index('rows')
        table, table_rows = dft_tables(img_size, row_devs)
        table = jnp.asarray(table)
        table_rows = jnp.asarray(table_rows)

        valid = jnp.arange(samples, dtype=jnp.int32)[None, :] < counts[0]
        place = jnp.clip(row_idx - me * block_rows, 0, block_rows - 1) + (SUB - 3)
        col0 = lax.rem(jnp.clip(col_idx, 0, cols - 1) + (cols - 3), cols)
        addr = (place // SUB) * pitch + col0
        packed = jnp.concatenate([
            kspace.reshape(16, samples),
            jnp.where(valid, weight_row, 0.0),
            (place % SUB).astype(F32)[None, :],
            jnp.zeros((1, samples), F32),
            weight_col,
            addr.astype(F32)[None, :],
            jnp.broadcast_to(counts[0].astype(F32), (1, samples)),
        ], axis=0)
        swap = [(p, (p + row_devs // 2) % row_devs) for p in range(row_devs)]
        packed_other = lax.ppermute(packed, 'rows', swap)

        def grid_block(data):
            return pl.pallas_call(
                functools.partial(grid_kernel, pitch=pitch, cols=cols),
                out_shape=(jax.ShapeDtypeStruct((2, 16, block_rows - 16, LANES), BF16), jax.ShapeDtypeStruct((3, cols, LANES), F32)),
                in_specs=[pl.BlockSpec(memory_space=pltpu.VMEM), pl.BlockSpec(memory_space=pl.ANY)],
                out_specs=(pl.BlockSpec(memory_space=pltpu.VMEM), pl.BlockSpec(memory_space=pltpu.VMEM)),
                scratch_shapes=[
                    pltpu.VMEM((groups * pitch, LANES), F32),
                    pltpu.VMEM((groups * pitch, LANES), F32),
                    pltpu.VMEM((LANES, 2 * LANES), F32),
                    pltpu.VMEM((SUB, samples), jnp.int32),
                    pltpu.VMEM((cols, 2 * LANES), BF16),
                    pltpu.VMEM((2, 2 * half, cols), BF16),
                    pltpu.SMEM((SUB, samples), jnp.int32),
                    pltpu.SemaphoreType.DMA,
                    pltpu.SemaphoreType.DMA,
                ],
                compiler_params=pltpu.CompilerParams(vmem_limit_bytes=40 * 1024 * 1024),
                cost_estimate=pl.CostEstimate(flops=4_000_000_000, bytes_accessed=4_000_000, transcendentals=0),
                name='grid_block',
            )(data, table)

        h_own, e_own = grid_block(packed)
        h_oth, e_oth = grid_block(packed_other)
        any_spec = pl.BlockSpec(memory_space=pl.ANY)
        vmem_spec = pl.BlockSpec(memory_space=pltpu.VMEM)
        return pl.pallas_call(
            image_kernel,
            out_shape=jax.ShapeDtypeStruct((2, half, img_size), F32),
            in_specs=[any_spec] * 7 + [vmem_spec] * 2,
            out_specs=vmem_spec,
            scratch_shapes=[
                pltpu.VMEM((2, 2, cols, LANES), F32),
                pltpu.VMEM((2, cols, LANES), F32),
                pltpu.VMEM((cols, 2 * LANES), BF16),
                pltpu.VMEM((2, 2, 16, 2 * SUB, LANES), BF16),
                pltpu.VMEM((2, 2 * half, cols), BF16),
                pltpu.VMEM((2, 2, img_size, cols // 2), BF16),
                pltpu.VMEM((2, 8, img_size, half), F32),
                pltpu.VMEM((2, 16, 2 * block_rows, LANES), BF16),
                pltpu.VMEM((2, img_size, half), F32),
                pltpu.VMEM((4, 2, half, half), F32),
                pltpu.SemaphoreType.DMA((5,)),
                pltpu.SemaphoreType.DMA((2,)),
                pltpu.SemaphoreType.DMA((2,)),
                pltpu.SemaphoreType.DMA((2,)),
                pltpu.SemaphoreType.DMA((2,)),
                pltpu.SemaphoreType.DMA((2,)),
                pltpu.SemaphoreType.DMA((2,)),
                pltpu.SemaphoreType.DMA((2,)),
                pltpu.SemaphoreType.DMA((3,)),
                pltpu.SemaphoreType.DMA((3,)),
            ],
            compiler_params=pltpu.CompilerParams(collective_id=0, has_side_effects=True, vmem_limit_bytes=40 * 1024 * 1024),
            cost_estimate=pl.CostEstimate(flops=6_000_000_000, bytes_accessed=8_000_000, transcendentals=0),
            name='image_block',
        )(h_own, h_oth, e_own, e_oth, table, table_rows, coil_maps, deapod[:, None], deapod[None, :])

    spec_samples = P(None, part_axes)
    in_specs = (P(None, None, part_axes), spec_samples, spec_samples, P(part_axes), P(part_axes), P(part_axes), P(None, None, None, part_axes), P())
    return jax.shard_map(local_step, mesh=mesh, in_specs=in_specs, out_specs=P(None, part_axes, None), check_vma=False)
```

profile of v0, /device:TPU:0, one launch (start us, length us, event | category | flops | bytes accessed | tf_op | source)
XLA Modules:
  0.0 56.0 jit_solution(16327667903208724987)
XLA Ops:
  0.7 0.8 %broadcast_select_fusion = f32[6,1024]{1,0:T(8,128)S(1)} fusion(f32[6,1024]{1,0:T(8,128)} %param.11, pred[1024]{0:T(1024)(128)(4,1)S(1)} %iota_compare_fusion), kind=kLoop, calls=%fused_computation | loop fusion | flops 6144 | bytes 50176 | tf_op jit(solution)/shard_map/jit(_where)/select_n | solution.py:270
  1.4 0.7 %fusion.3 = (f32[1024]{0:T(1024)S(1)}, f32[1024]{0:T(1024)S(1)}) fusion(s32[1024]{0:T(1024)} %param.14, s32[1024]{0:T(1024)} %param.13, s32[]{:T(128)S(6)} %mul.9), kind=kLoop, calls=%fused_computation.9 | loop fusion | flops 29696 | bytes 16388 | tf_op jit(solution)/shard_map/convert_element_type | solution.py:274
  2.2 1.7 %concatenate.3.data_ref = f32[32,1024]{1,0:T(8,128)S(1)} concatenate(f32[16,1024]{1,0:T(8,128)} %bitcast.6, f32[6,1024]{1,0:T(8,128)S(1)} %broadcast_select_fusion, f32[1,1024]{1,0:T(1,128)S(1)} %bitcast.8, f32[1,1024]{1,0:T(1,128)S(1)} %broadcast_in_dim.34, f32[6,1024]{1,0:T(8,128)} %param.12, f32[1,1024]{1,0:T(1,128)S(1)} %bitcast.7, f32[1,1024]{1,0:T(1,128)S(1)} %broadcast_in_dim.36), dimensions={0} | concatenate | bytes 262144 | tf_op jit(solution)/shard_map/concatenate | solution.py:268
  3.8 3.4 %collective-permute-start = (f32[32,1024]{1,0:T(8,128)S(1)}, f32[32,1024]{1,0:T(8,128)}, u32[]{:S(2)}, u32[]{:S(2)}) collective-permute-start(f32[32,1024]{1,0:T(8,128)S(1)} %concatenate.3.data_ref), channel_id=1, source_target_pairs={{0,2},{1,3},{2,0},{3,1},{4,6},{5,7},{6,4},{7,5}} | collective-permute-start | bytes 393224 | tf_op jit(solution)/shard_map/ppermute | solution.py:278
  7.2 0.0 copy-start
  7.2 1.3 %copy-done = bf16[2,384,768]{2,1,0:T(8,128)(2,1)S(1)} copy-done((bf16[2,384,768]{2,1,0:T(8,128)(2,1)S(1)}, bf16[2,384,768]{2,1,0:T(8,128)(2,1)}, u32[]{:S(2)}) %copy-start) | copy-done | bytes 1179672
  8.5 0.0 copy-start.7
  8.5 9.9 %grid_block.2 = (bf16[2,16,176,128]{3,2,1,0:T(8,128)(2,1)S(1)}, f32[3,768,128]{2,1,0:T(8,128)S(1)}) custom-call(f32[32,1024]{1,0:T(8,128)S(1)} %concatenate.3.data_ref, bf16[2,384,768]{2,1,0:T(8,128)(2,1)S(1)} %copy-done), custom_call_target="tpu_custom_call" | custom-call | flops 4000000000 | bytes 4000000 | tf_op jit(solution)/shard_map/grid_block/pallas_call | solution.py:281
  18.3 0.0 copy-start.3
  18.3 1.1 %copy-done.3 = bf16[2,16,176,128]{3,2,1,0:T(8,128)(2,1)} copy-done((bf16[2,16,176,128]{3,2,1,0:T(8,128)(2,1)}, bf16[2,16,176,128]{3,2,1,0:T(8,128)(2,1)S(1)}, u32[]{:S(2)}) %copy-start.3) | copy-done | bytes 1441816
  19.5 0.0 copy-start.5
  19.5 1.0 %copy-done.5 = f32[3,768,128]{2,1,0:T(8,128)} copy-done((f32[3,768,128]{2,1,0:T(8,128)}, f32[3,768,128]{2,1,0:T(8,128)S(1)}, u32[]{:S(2)}) %copy-start.5) | copy-done | bytes 1179672
  20.5 0.0 copy-done.7
  20.5 0.1 broadcast_in_dim.39.dcol_ref
  20.6 2.2 %copy.12.maps_hbm = f32[2,8,384,96]{3,2,1,0:T(8,128)S(1)} copy(f32[2,8,384,96]{2,3,1,0:T(8,128)} %param.16) | data formatting | bytes 4718592 | tf_op args[6]
  22.8 0.0 collective-permute-done.data_ref
  22.9 0.0 copy-start.1
  22.9 1.3 %copy-done.1 = bf16[2,384,768]{2,1,0:T(8,128)(2,1)S(1)} copy-done((bf16[2,384,768]{2,1,0:T(8,128)(2,1)S(1)}, bf16[2,384,768]{2,1,0:T(8,128)(2,1)}, u32[]{:S(2)}) %copy-start.1) | copy-done | bytes 1179672
  24.1 0.0 copy-start.2
  24.1 0.0 copy-start.4
  24.1 0.0 copy-start.6
  24.1 13.2 %grid_block.3 = (bf16[2,16,176,128]{3,2,1,0:T(8,128)(2,1)S(1)}, f32[3,768,128]{2,1,0:T(8,128)S(1)}) custom-call(f32[32,1024]{1,0:T(8,128)} %collective-permute-done.data_ref, bf16[2,384,768]{2,1,0:T(8,128)(2,1)S(1)} %copy-done.1), custom_call_target="tpu_custom_call" | custom-call | flops 4000000000 | bytes 4000000 | tf_op jit(solution)/shard_map/grid_block/pallas_call | solution.py:281
  37.3 0.0 copy-done.2
  37.3 0.0 copy-done.4
  37.4 0.0 copy-done.6
  37.4 17.9 %image_block.1 = f32[2,96,384]{2,1,0:T(8,128)S(1)} custom-call(bf16[2,16,176,128]{3,2,1,0:T(8,128)(2,1)S(1)} %copy-done.4, bf16[2,16,176,128]{3,2,1,0:T(8,128)(2,1)S(1)} %get-tuple-element.10.h_oth, f32[3,768,128]{2,1,0:T(8,128)S(1)} %copy-done.6, f32[3,768,128]{2,1,0:T(8,128)S(1)} %get-tuple-element.12.e_oth, bf16[2,384,768]{2,1,0:T(8,128)(2,1)S(1)} %copy-done.1, ...), custom_call_target="tpu_custom_call" | custom-call | flops 6000000000 | bytes 8000000 | tf_op jit(solution)/shard_map/image_block/pallas_call | solution.py:306
  55.2 0.7 %copy.16 = f32[2,96,384]{2,1,0:T(8,128)} copy(f32[2,96,384]{2,1,0:T(8,128)S(1)} %image_block.1) | data formatting | bytes 589824
  (4 shorter events, 0.0 us)
Async XLA Ops:
  3.8 19.0 %collective-permute-start = (f32[32,1024]{1,0:T(8,128)S(1)}, f32[32,1024]{1,0:T(8,128)}, u32[]{:S(2)}, u32[]{:S(2)}) collective-permute-start(f32[32,1024]{1,0:T(8,128)S(1)} %concatenate.3.data_ref), channel_id=1, source_target_pairs={{0,2},{1,3},{2,0},{3,1},{4,6},{5,7},{6,4},{7,5}} | collective-permute-start | bytes 393224 | tf_op jit(solution)/shard_map/ppermute | solution.py:278
  7.2 1.3 %copy-start = (bf16[2,384,768]{2,1,0:T(8,128)(2,1)S(1)}, bf16[2,384,768]{2,1,0:T(8,128)(2,1)}, u32[]{:S(2)}) copy-start(bf16[2,384,768]{2,1,0:T(8,128)(2,1)} %constant.54.clone.tab_hbm) | copy-start | bytes 3538948
  8.5 12.0 %copy-start.7 = (f32[384]{0:T(512)S(1)}, f32[384]{0:T(512)}, u32[]{:S(2)}) copy-start(f32[384]{0:T(512)} %param.17) | copy-start | bytes 4612
  18.3 1.1 %copy-start.3 = (bf16[2,16,176,128]{3,2,1,0:T(8,128)(2,1)}, bf16[2,16,176,128]{3,2,1,0:T(8,128)(2,1)S(1)}, u32[]{:S(2)}) copy-start(bf16[2,16,176,128]{3,2,1,0:T(8,128)(2,1)S(1)} %get-tuple-element.9.h_own) | copy-start | bytes 4325380
  19.5 1.0 %copy-start.5 = (f32[3,768,128]{2,1,0:T(8,128)}, f32[3,768,128]{2,1,0:T(8,128)S(1)}, u32[]{:S(2)}) copy-start(f32[3,768,128]{2,1,0:T(8,128)S(1)} %get-tuple-element.11.e_own) | copy-start | bytes 3538948
  22.9 1.3 %copy-start.1 = (bf16[2,384,768]{2,1,0:T(8,128)(2,1)S(1)}, bf16[2,384,768]{2,1,0:T(8,128)(2,1)}, u32[]{:S(2)}) copy-start(bf16[2,384,768]{2,1,0:T(8,128)(2,1)} %constant.54.clone.tab_hbm) | copy-start | bytes 3538948
  24.1 13.2 %copy-start.2 = (bf16[2,2,384,384]{3,2,1,0:T(8,128)(2,1)S(1)}, bf16[2,2,384,384]{3,2,1,0:T(8,128)(2,1)}, u32[]{:S(2)}) copy-start(bf16[2,2,384,384]{3,2,1,0:T(8,128)(2,1)} %constant.55.clone.tab2_hbm) | copy-start | bytes 3538948
  24.1 13.2 %copy-start.4 = (bf16[2,16,176,128]{3,2,1,0:T(8,128)(2,1)S(1)}, bf16[2,16,176,128]{3,2,1,0:T(8,128)(2,1)}, u32[]{:S(2)}) copy-start(bf16[2,16,176,128]{3,2,1,0:T(8,128)(2,1)} %copy-done.3) | copy-start | bytes 4325380
  24.1 13.2 %copy-start.6 = (f32[3,768,128]{2,1,0:T(8,128)S(1)}, f32[3,768,128]{2,1,0:T(8,128)}, u32[]{:S(2)}) copy-start(f32[3,768,128]{2,1,0:T(8,128)} %copy-done.5) | copy-start | bytes 3538948
where the time goes:
time: 56.4 us; the launch traced here: 56 us
  Pallas kernels  40.9 us (73%)
  local copies, waits for them, and re-layouts  9.42 us (17%)
  starting transfers between devices  3.36 us (6%)
  other arithmetic  1.49 us (3%)
  between operations  0.77 us (1%)
    pallas_call x2, Pallas kernels, grid_block(): pl.pallas_call(functools.partial(grid_kernel, pitch=pitch, cols=cols), ou...  23 us
    pallas_call x1, Pallas kernels, local_step(): pl.pallas_call(image_kernel, out_shape=jax.ShapeDtypeStruct((2, half, img...  17.9 us
    unnamed x18, local copies, waits for them, and re-layouts  7.64 us
    ppermute x1, starting transfers between devices, local_step(): packed_other = lax.ppermute(packed, 'rows', swap)  3.36 us
    concatenate x1, local copies, waits for them, and re-layouts, local_step(): jnp.concatenate([kspace.reshape(16, samples), jnp.where(valid, weight_row...  1.66 us
  transfers between devices with their start and end apart: 1, of which 0 were waited for; matrix products, arithmetic and copies ran while one was open for 4% of the time, Pallas kernels for 18%

commit v1 on v0

v1 whole, which is shorter than its diff:
```python
import functools
import math

import jax
import jax.numpy as jnp
import numpy as np
from jax import lax
from jax.experimental import pallas as pl
from jax.experimental.pallas import tpu as pltpu
from jax.sharding import PartitionSpec as P

MESH = pl.DeviceIdType.MESH
F32 = jnp.float32
BF16 = jnp.bfloat16
LANES = 128
SUB = 8


def dft_tables(img_size, row_devs):
    grid_size = 2 * img_size
    frequency = np.arange(grid_size)[None, :] - img_size
    pixel_pos = np.arange(img_size)[:, None] - img_size // 2
    angle = ((frequency * pixel_pos) % grid_size).astype(np.float64) * (2.0 * math.pi / grid_size)
    table = np.stack([np.cos(angle), np.sin(angle)]).astype(np.float32).astype(jnp.bfloat16)
    block = grid_size // row_devs
    order = np.concatenate([np.arange(SUB, block - SUB), np.arange(SUB), np.arange(block - SUB, block)])
    by_core = []
    for core in range(2):
        rows = np.concatenate([(2 * chip + core) * block + order for chip in range(row_devs // 2)])
        by_core.append(table[:, :, rows])
    by_core = np.stack(by_core)
    by_half = by_core.reshape(2, 2, 2, img_size // 2, grid_size // 2).transpose(0, 2, 1, 3, 4)
    return table, np.ascontiguousarray(by_half.reshape(2, 2, img_size, grid_size // 2))


def pack_kernel(ks_ref, wr_ref, wc_ref, row_ref, col_ref, count_ref, out_ref, *, block_rows, pitch, cols):
    start = lax.axis_index('rows') * block_rows
    count = count_ref[0]
    samples = ks_ref.shape[1]
    valid = lax.broadcasted_iota(jnp.int32, (6, samples), 1) < count
    place = jnp.clip(row_ref[...] - start, 0, block_rows - 1) + (SUB - 3)
    col0 = jnp.clip(col_ref[...], 0, cols - 1) - 3
    col0 = jnp.where(col0 < 0, col0 + cols, col0)
    group = lax.shift_right_logical(place, 3)
    addr = group * pitch + col0
    offset = place - group * SUB
    out_ref[0:16, :] = ks_ref[...]
    out_ref[16:24, :] = jnp.concatenate([jnp.where(valid, wr_ref[...], 0.0), offset.astype(F32), jnp.zeros((1, samples), F32)], axis=0)
    out_ref[24:32, :] = jnp.concatenate([wc_ref[...], addr.astype(F32), jnp.full((1, samples), count, jnp.int32).astype(F32)], axis=0)


def grid_kernel(data_ref, g_ref, edge_ref, acc_a, acc_b, lvec, addr_v, addr_s, addr_sem, *, pitch, cols):
    groups = acc_a.shape[0] // pitch
    addr_v[...] = data_ref[24:32, :].astype(jnp.int32)
    addr_copy = pltpu.make_async_copy(addr_v, addr_s, addr_sem)
    addr_copy.start()

    @pl.loop(0, groups)
    def _(g):
        base = pl.multiple_of(g * pitch, SUB)
        acc_a[pl.ds(base, pitch), :] = jnp.zeros((pitch, LANES), F32)
        acc_b[pl.ds(base, pitch), :] = jnp.zeros((pitch, LANES), F32)

    addr_copy.wait()
    count = addr_s[7, 0]
    slot = lax.broadcasted_iota(jnp.int32, (2 * SUB, LANES), 0).astype(F32)
    tap_row = lax.broadcasted_iota(jnp.int32, (SUB, LANES), 0)

    @pl.loop(0, (count + LANES - 1) // LANES)
    def _(blk):
        first = pl.multiple_of(blk * LANES, LANES)
        wr8 = data_ref[16:24, pl.ds(first, LANES)]
        tap = slot - wr8[6:7, :]
        wrs = jnp.where(tap == 0.0, wr8[0:1, :], 0.0)
        for a in range(1, 6):
            wrs = wrs + jnp.where(tap == float(a), wr8[a:a + 1, :], 0.0)
        y16 = data_ref[0:16, pl.ds(first, LANES)]
        for part in range(2):
            w_part = wrs[part * SUB:(part + 1) * SUB, :]
            full = jnp.concatenate([y16[ch:ch + 1, :] * w_part for ch in range(16)], axis=0)
            lvec[:, part * LANES:(part + 1) * LANES] = full.T
        wc8 = jnp.where(tap_row < 6, data_ref[24:32, pl.ds(first, LANES)], 0.0)

        def contribution(k):
            wide = jnp.broadcast_to(wc8[:, k:k + 1], (SUB, LANES))
            lo = jnp.broadcast_to(lvec[k:k + 1, 0:LANES], (SUB, LANES))
            hi = jnp.broadcast_to(lvec[k:k + 1, LANES:2 * LANES], (SUB, LANES))
            return wide * lo, wide * hi

        for k in range(0, LANES, 2):
            at_a = addr_s[6, first + k]
            at_b = addr_s[6, first + k + 1]
            a_lo, a_hi = contribution(k)
            b_lo, b_hi = contribution(k + 1)
            old_a_lo = acc_a[pl.ds(at_a, SUB), :]
            old_a_hi = acc_a[pl.ds(at_a + pitch, SUB), :]
            old_b_lo = acc_b[pl.ds(at_b, SUB), :]
            old_b_hi = acc_b[pl.ds(at_b + pitch, SUB), :]
            acc_a[pl.ds(at_a, SUB), :] = old_a_lo + a_lo
            acc_a[pl.ds(at_a + pitch, SUB), :] = old_a_hi + a_hi
            acc_b[pl.ds(at_b, SUB), :] = old_b_lo + b_lo
            acc_b[pl.ds(at_b + pitch, SUB), :] = old_b_hi + b_hi

    def rows_sum(g, start, size):
        at = pl.multiple_of(g * pitch + start, SUB)
        total = acc_a[pl.ds(at, size), :] + acc_b[pl.ds(at, size), :]
        if start == 0:
            wrap = pl.multiple_of(g * pitch + cols, SUB)
            head = total[0:SUB] + (acc_a[pl.ds(wrap, SUB), :] + acc_b[pl.ds(wrap, SUB), :])
            total = jnp.concatenate([head, total[SUB:]], axis=0)
        return total

    chunk = 128
    for start in range(0, cols, chunk):
        edge_ref[0, start:start + chunk, :] = rows_sum(1, start, chunk)
        edge_ref[1, start:start + chunk, :] = rows_sum(groups - 2, start, chunk)
        edge_ref[2, start:start + chunk, :] = rows_sum(0, start, chunk) + rows_sum(groups - 1, start, chunk)

    @pl.loop(0, (groups - 4) // 2)
    def _(pair):
        for start in range(0, cols, chunk):
            for side in range(2):
                g_ref[pair, start:start + chunk, side * LANES:(side + 1) * LANES] = rows_sum(2 + 2 * pair + side, start, chunk).astype(BF16)


def image_kernel(g_own, g_oth, e_own, e_oth, tab_ref, tab2_v, maps_r, dcol_ref, drow_ref, out_ref,
                 margins, gbuf_a, gbuf_b, pbuf_a, pbuf_b, tab_v, maps_v, h_all, h_send, img, pieces,
                 m_send, m_recv, s_send, s_recv, p_send, p_recv):
    me = lax.axis_index('rows')
    chip = me // 2
    core = me % 2
    peers = [2 * chip + 1 - core, 2 * (1 - chip) + core, 2 * (1 - chip) + 1 - core]
    partner = {'rows': peers[0]}
    block = h_all.shape[2] // 2
    pairs = g_own.shape[0]
    inner = 2 * SUB * pairs
    half = img.shape[2]
    cols = g_own.shape[1]

    barrier = pltpu.get_barrier_semaphore()
    for peer in peers:
        pl.semaphore_signal(barrier, inc=1, device_id={'rows': peer}, device_id_type=MESH)
    pl.semaphore_wait(barrier, 3)

    m_copies = [pltpu.make_async_remote_copy(src_ref=e.at[2], dst_ref=margins.at[s], send_sem=m_send.at[s], recv_sem=m_recv.at[s], device_id=partner, device_id_type=MESH) for s, e in enumerate((e_own, e_oth))]
    for copy in m_copies:
        copy.start()

    for part in range(2):
        for side, owner in enumerate((me, peers[0])):
            tab_v[(2 * part + side) * half:(2 * part + side + 1) * half, :] = tab_ref[part, pl.ds(pl.multiple_of(owner * half, 2 * SUB), half), :]

    places = [pl.multiple_of(chip * block, 2 * SUB), pl.multiple_of((1 - chip) * block, 2 * SUB)]
    lane = lax.broadcasted_iota(jnp.int32, (half, LANES), 1)
    sign = jnp.where(lane < LANES // 2, -1.0, 1.0).astype(F32)

    def dot_pair(grid, pbuf):
        pbuf[...] = jnp.dot(tab_v[...], grid, preferred_element_type=F32)

    def turn_pair(pbuf, slot, row):
        for j_half in range(2):
            turned = []
            for side in range(2):
                lanes = slice(side * LANES, (side + 1) * LANES)
                by_cos = pbuf[j_half * half:(j_half + 1) * half, lanes]
                by_sin = pbuf[(2 + j_half) * half:(3 + j_half) * half, lanes]
                mixed = by_cos + sign * pltpu.roll(by_sin, LANES // 2, 1)
                mixed = jnp.concatenate([mixed, jnp.zeros((LANES - half, LANES), F32)], axis=0)
                turned.append(mixed.T)
            for ch in range(16):
                rows = slice(ch * SUB, (ch + 1) * SUB)
                tile = jnp.concatenate([turned[0][rows], turned[1][rows]], axis=0).astype(BF16)
                if j_half == 0:
                    h_all[core, ch, pl.ds(pl.multiple_of(places[slot] + row, 2 * SUB), 2 * SUB), :] = tile
                else:
                    h_send[slot, ch, pl.ds(pl.multiple_of(row, 2 * SUB), 2 * SUB), :] = tile

    sends = []

    def send_rows(slot, start, size):
        n = len(sends)
        src = h_send.at[slot, :, start:start + size, :]
        dst = h_all.at[core, :, pl.ds(pl.multiple_of(places[slot] + start, 2 * SUB), size), :]
        copy = pltpu.make_async_remote_copy(src_ref=src, dst_ref=dst, send_sem=s_send.at[n], recv_sem=s_recv.at[n], device_id=partner, device_id_type=MESH)
        copy.start()
        sends.append(copy)

    def close_margins():
        for copy in m_copies:
            copy.wait()
        low = lane[:1] % SUB < SUB // 2
        for s, (e, gbuf) in enumerate(((e_own, gbuf_a), (e_oth, gbuf_b))):
            from_low = lax.rem(s + 1 - core, 2)
            from_high = lax.rem(s + core, 2)
            for start in range(0, cols, 128):
                rows = slice(start, start + 128)
                gbuf[rows, 0:LANES] = (e[0, rows, :] + jnp.where(low, margins[from_low, rows, :], 0.0)).astype(BF16)
                gbuf[rows, LANES:2 * LANES] = (e[1, rows, :] + jnp.where(low, 0.0, margins[from_high, rows, :])).astype(BF16)

    steps = [(g_own, pair, 0, 2 * SUB * pair) for pair in range(pairs)]
    steps += [(gbuf_a, None, 0, inner), (gbuf_b, None, 1, inner)]
    steps += [(g_oth, pair, 1, 2 * SUB * pair) for pair in range(pairs)]
    maps_left = [(q, coil, start) for coil in range(8) for q in range(2) for start in range(0, maps_r.shape[3], LANES)]
    split = 5
    after = {pairs: [(0, 0, inner + 2 * SUB)], pairs + 1 + split: [(1, inner, 2 * SUB), (1, 0, 2 * SUB * split)], 2 * pairs + 1: [(1, 2 * SUB * split, inner - 2 * SUB * split)]}
    bufs = (pbuf_a, pbuf_b)

    def turn_step(n):
        turn_pair(bufs[n % 2], steps[n][2], steps[n][3])
        for where in after.get(n, ()):
            send_rows(*where)

    for n, (grid, pair, slot, row) in enumerate(steps):
        if n == pairs:
            close_margins()
        dot_pair(grid[...] if pair is None else grid[pair], bufs[n % 2])
        for q, coil, start in maps_left[2 * n:2 * n + 2]:
            maps_v[q, coil, start:start + LANES, :] = maps_r[q, coil, :, start:start + LANES].T
        if n:
            turn_step(n - 1)
    turn_step(len(steps) - 1)

    rows_half = 2 * half

    def row_pass(parities, i_half):
        place = pl.ds(pl.multiple_of(i_half * rows_half, rows_half), rows_half)

        def combine(coil):
            pbuf = bufs[coil % 2]
            img_re = (pbuf[:rows_half, :LANES] - pbuf[rows_half:, LANES:])[:, :half]
            img_im = (pbuf[rows_half:, :LANES] + pbuf[:rows_half, LANES:])[:, :half]
            map_re = maps_v[0, coil, place, :]
            map_im = maps_v[1, coil, place, :]
            img[0, place, :] += map_re * img_re + map_im * img_im
            img[1, place, :] += map_re * img_im - map_im * img_re

        for coil in range(8):
            both = 0.0
            for parity in parities:
                field = jnp.concatenate([h_all[parity, coil], h_all[parity, coil + 8]], axis=1)
                both += jnp.dot(tab2_v[parity, i_half], field, preferred_element_type=F32)
            bufs[coil % 2][...] = both
            if coil:
                combine(coil - 1)
        combine(7)

    img[...] = jnp.zeros_like(img)
    row_pass([core], 1 - chip)
    for copy in sends:
        copy.wait()
    p_copies = []

    def send_piece(rel):
        target = peers[rel - 1]
        copy = pltpu.make_async_remote_copy(src_ref=img.at[:, pl.ds(pl.multiple_of(target * half, SUB), half), :], dst_ref=pieces.at[rel], send_sem=p_send.at[rel - 1], recv_sem=p_recv.at[rel - 1], device_id={'rows': target}, device_id_type=MESH)
        copy.start()
        p_copies.append(copy)

    row_pass([1 - core], 1 - chip)
    send_piece(2)
    send_piece(3)
    row_pass([core, 1 - core], chip)
    send_piece(1)
    pieces[0] = img[:, pl.ds(pl.multiple_of(me * half, SUB), half), :]
    for copy in p_copies:
        copy.wait()
    scale = dcol_ref[pl.ds(pl.multiple_of(me * half, SUB), half), :] * drow_ref[...]
    for q in range(2):
        row = []
        for src in range(4):
            rel = lax.rem(src // 2 + chip, 2) * 2 + lax.rem(src % 2 + core, 2)
            row.append(pieces[rel, q])
        out_ref[q] = jnp.concatenate(row, axis=1) * scale


def solution(mesh):
    row_devs = mesh.shape['rows']
    part_axes = ('exam', 'rows')

    def local_step(kspace, weight_row, weight_col, row_idx, col_idx, counts, coil_maps, deapod):
        img_size = deapod.shape[0]
        cols = 2 * img_size
        block_rows = cols // row_devs
        samples = kspace.shape[2]
        pitch = cols + SUB
        half = img_size // row_devs
        groups = block_rows // SUB + 2
        pairs = (groups - 4) // 2
        table, table_rows = dft_tables(img_size, row_devs)
        table = jnp.asarray(table)
        table_rows = jnp.asarray(table_rows)
        vmem_spec = pl.BlockSpec(memory_space=pltpu.VMEM)
        smem_spec = pl.BlockSpec(memory_space=pltpu.SMEM)

        packed = pl.pallas_call(
            functools.partial(pack_kernel, block_rows=block_rows, pitch=pitch, cols=cols),
            out_shape=jax.ShapeDtypeStruct((32, samples), F32),
            in_specs=[vmem_spec] * 5 + [smem_spec],
            out_specs=vmem_spec,
            compiler_params=pltpu.CompilerParams(vmem_limit_bytes=2 * 1024 * 1024),
            name='pack_block',
        )(kspace.reshape(16, samples), weight_row, weight_col, row_idx[None, :], col_idx[None, :], counts)
        swap = [(p, (p + row_devs // 2) % row_devs) for p in range(row_devs)]
        packed_other = lax.ppermute(packed, 'rows', swap)

        def grid_block(data):
            return pl.pallas_call(
                functools.partial(grid_kernel, pitch=pitch, cols=cols),
                out_shape=(jax.ShapeDtypeStruct((pairs, cols, 2 * LANES), BF16), jax.ShapeDtypeStruct((3, cols, LANES), F32)),
                in_specs=[vmem_spec],
                out_specs=(vmem_spec, vmem_spec),
                scratch_shapes=[
                    pltpu.VMEM((groups * pitch, LANES), F32),
                    pltpu.VMEM((groups * pitch, LANES), F32),
                    pltpu.VMEM((LANES, 2 * LANES), F32),
                    pltpu.VMEM((SUB, samples), jnp.int32),
                    pltpu.SMEM((SUB, samples), jnp.int32),
                    pltpu.SemaphoreType.DMA,
                ],
                compiler_params=pltpu.CompilerParams(vmem_limit_bytes=28 * 1024 * 1024),
                cost_estimate=pl.CostEstimate(flops=4_000_000_000, bytes_accessed=4_000_000, transcendentals=0),
                name='grid_block',
            )(data)

        g_own, e_own = grid_block(packed)
        g_oth, e_oth = grid_block(packed_other)
        dma = pltpu.SemaphoreType.DMA
        return pl.pallas_call(
            image_kernel,
            out_shape=jax.ShapeDtypeStruct((2, half, img_size), F32),
            in_specs=[vmem_spec] * 9,
            out_specs=vmem_spec,
            scratch_shapes=[
                pltpu.VMEM((2, cols, LANES), F32),
                pltpu.VMEM((cols, 2 * LANES), BF16),
                pltpu.VMEM((cols, 2 * LANES), BF16),
                pltpu.VMEM((4 * half, 2 * LANES), F32),
                pltpu.VMEM((4 * half, 2 * LANES), F32),
                pltpu.VMEM((4 * half, cols), BF16),
                pltpu.VMEM((2, 8, img_size, half), F32),
                pltpu.VMEM((2, 16, 2 * block_rows, LANES), BF16),
                pltpu.VMEM((2, 16, block_rows, LANES), BF16),
                pltpu.VMEM((2, img_size, half), F32),
                pltpu.VMEM((4, 2, half, half), F32),
                dma((2,)), dma((2,)), dma((4,)), dma((4,)), dma((3,)), dma((3,)),
            ],
            compiler_params=pltpu.CompilerParams(collective_id=0, has_side_effects=True, vmem_limit_bytes=32 * 1024 * 1024),
            cost_estimate=pl.CostEstimate(flops=6_000_000_000, bytes_accessed=8_000_000, transcendentals=0),
            name='image_block',
        )(g_own, g_oth, e_own, e_oth, table, table_rows, jnp.swapaxes(coil_maps, 2, 3), deapod[:, None], deapod[None, :])

    spec_samples = P(None, part_axes)
    in_specs = (P(None, None, part_axes), spec_samples, spec_samples, P(part_axes), P(part_axes), P(part_axes), P(None, None, None, part_axes), P())
    return jax.shard_map(local_step, mesh=mesh, in_specs=in_specs, out_specs=P(None, part_axes, None), check_vma=False)
```

time: 56.4 us -> 36.1 us (0.64)
  Pallas kernels: 40.9 us -> 27.3 us
  local copies, waits for them, and re-layouts: 9.42 us -> 4.57 us
  other arithmetic: 1.49 us -> 0 us
    pallas_call x2, Pallas kernels: 23 us -> 11.1 us  [grid_block(): pl.pallas_call(functools.partial(grid_kernel, pitch=pitch, cols=cols), ou...]
    unnamed x18 -> x19, local copies, waits for them, and re-layouts: 7.64 us -> 4.46 us
    concatenate x1 -> x0, local copies, waits for them, and re-layouts: 1.66 us -> none  [local_step(): jnp.concatenate([kspace.reshape(16, samples), jnp.where(valid, weight_row...]
    pallas_call x1, Pallas kernels: 17.9 us -> 16.2 us  [local_step(): pl.pallas_call(image_kernel, out_shape=jax.ShapeDtypeStruct((2, half, img...]
    select_n x1 -> x0, other arithmetic: 0.77 us -> none  [local_step(): jnp.where(valid, weight_row, 0.0)]
    convert_element_type x1 -> x0, other arithmetic: 0.72 us -> none  [local_step(): addr.astype(F32)[None, :]]
  transfers between devices with their start and end apart: 1 -> 1, of which waited for: 0 -> 0; matrix products, arithmetic and copies ran while one was open for 4% -> 0% of each run, Pallas kernels for 18% -> 13%
where the time goes in v1:
time: 36.1 us; the launch traced here: 36 us
  Pallas kernels  27.3 us (76%)
  local copies, waits for them, and re-layouts  4.57 us (13%)
  starting transfers between devices  3.36 us (9%)
  between operations  0.78 us (2%)
    pallas_call x1, Pallas kernels, local_step(): pl.pallas_call(image_kernel, out_shape=jax.ShapeDtypeStruct((2, half, img...  16.2 us
    pallas_call x2, Pallas kernels, grid_block(): pl.pallas_call(functools.partial(grid_kernel, pitch=pitch, cols=cols), ou...  11.1 us
    unnamed x19, local copies, waits for them, and re-layouts  4.46 us
    ppermute x1, starting transfers between devices, local_step(): packed_other = lax.ppermute(packed, 'rows', swap)  3.36 us
  transfers between devices with their start and end apart: 1, of which 0 were waited for; matrix products, arithmetic and copies ran while one was open for 0% of the time, Pallas kernels for 13%

profile of v1, /device:TPU:0, one launch (start us, length us, event | category | flops | bytes accessed | tf_op | source)
XLA Modules:
  0.0 36.0 jit_solution(15277016652573680898)
XLA Ops:
  0.7 0.0 copy-start
  0.7 0.8 %copy-done = f32[2,8,1024]{2,1,0:T(8,128)S(1)} copy-done((f32[2,8,1024]{2,1,0:T(8,128)S(1)}, f32[2,8,1024]{2,1,0:T(8,128)}, u32[]{:S(2)}) %copy-start) | copy-done | bytes 65560
  1.5 0.0 copy-start.1
  1.5 0.8 %copy-done.1 = f32[6,1024]{1,0:T(8,128)S(1)} copy-done((f32[6,1024]{1,0:T(8,128)S(1)}, f32[6,1024]{1,0:T(8,128)}, u32[]{:S(2)}) %copy-start.1) | copy-done | bytes 24600
  2.3 0.0 copy-start.2
  2.3 0.8 %copy-done.2 = f32[6,1024]{1,0:T(8,128)S(1)} copy-done((f32[6,1024]{1,0:T(8,128)S(1)}, f32[6,1024]{1,0:T(8,128)}, u32[]{:S(2)}) %copy-start.2) | copy-done | bytes 24600
  3.0 0.0 copy-start.3
  3.0 0.7 %copy-done.3 = s32[1024]{0:T(1024)S(1)} copy-done((s32[1024]{0:T(1024)S(1)}, s32[1024]{0:T(1024)}, u32[]{:S(2)}) %copy-start.3) | copy-done | bytes 4120
  3.7 0.0 copy-start.4
  3.7 0.7 %copy-done.4 = s32[1024]{0:T(1024)S(1)} copy-done((s32[1024]{0:T(1024)S(1)}, s32[1024]{0:T(1024)}, u32[]{:S(2)}) %copy-start.4) | copy-done | bytes 4120
  4.4 0.0 copy-start.8
  4.4 3.4 %collective-permute-start = (f32[32,1024]{1,0:T(8,128)S(1)}, f32[32,1024]{1,0:T(8,128)S(1)}, u32[]{:S(2)}, u32[]{:S(2)}) collective-permute-start(f32[32,1024]{1,0:T(8,128)S(1)} %pack_block.1.data_ref), channel_id=1, source_target_pairs={{0,2},{1,3},{2,0},{3,1},{4,6},{5,7},{6,4},{7,5}} | collective-permute-start | bytes 393224 | tf_op jit(solution)/shard_map/ppermute | solution.py:304
  7.8 4.6 %grid_block.2 = (bf16[11,768,256]{2,1,0:T(8,128)(2,1)S(1)}, f32[3,768,128]{2,1,0:T(8,128)S(1)}) custom-call(f32[32,1024]{1,0:T(8,128)S(1)} %pack_block.1.data_ref), custom_call_target="tpu_custom_call" | custom-call | flops 4000000000 | bytes 4000000 | tf_op jit(solution)/shard_map/grid_block/pallas_call | solution.py:307
  12.4 0.0 copy-done.8
  12.4 0.1 broadcast_in_dim.16.dcol_ref
  12.5 0.0 copy-start.5
  12.5 0.0 copy-start.6
  12.6 0.0 copy-start.7
  12.6 0.0 collective-permute-done.data_ref
  12.6 6.5 %grid_block.3 = (bf16[11,768,256]{2,1,0:T(8,128)(2,1)S(1)}, f32[3,768,128]{2,1,0:T(8,128)S(1)}) custom-call(f32[32,1024]{1,0:T(8,128)S(1)} %collective-permute-done.data_ref), custom_call_target="tpu_custom_call" | custom-call | flops 4000000000 | bytes 4000000 | tf_op jit(solution)/shard_map/grid_block/pallas_call | solution.py:307
  19.0 0.0 copy-done.5
  19.0 0.0 copy-done.6
  19.1 0.0 copy-done.7
  19.1 16.2 %image_block.1 = f32[2,96,384]{2,1,0:T(8,128)S(1)} custom-call(bf16[11,768,256]{2,1,0:T(8,128)(2,1)S(1)} %get-tuple-element.9.g_own, bf16[11,768,256]{2,1,0:T(8,128)(2,1)S(1)} %get-tuple-element.10.g_oth, f32[3,768,128]{2,1,0:T(8,128)S(1)} %get-tuple-element.11.e_own, f32[3,768,128]{2,1,0:T(8,128)S(1)} %get-tuple-element.12.e_oth, ...), custom_call_target="tpu_custom_call" | custom-call | flops 6000000000 | bytes 8000000 | tf_op jit(solution)/shard_map/image_block/pallas_call | solution.py:328
  35.3 0.7 %copy.14 = f32[2,96,384]{2,1,0:T(8,128)} copy(f32[2,96,384]{2,1,0:T(8,128)S(1)} %image_block.1) | data formatting | bytes 589824
  (2 shorter events, 0.0 us)
Async XLA Ops:
  0.7 0.8 %copy-start = (f32[2,8,1024]{2,1,0:T(8,128)S(1)}, f32[2,8,1024]{2,1,0:T(8,128)}, u32[]{:S(2)}) copy-start(f32[2,8,1024]{2,1,0:T(8,128)} %param.10) | copy-start | bytes 196612
  1.5 0.8 %copy-start.1 = (f32[6,1024]{1,0:T(8,128)S(1)}, f32[6,1024]{1,0:T(8,128)}, u32[]{:S(2)}) copy-start(f32[6,1024]{1,0:T(8,128)} %wr_ref.1) | copy-start | bytes 73732
  2.3 0.8 %copy-start.2 = (f32[6,1024]{1,0:T(8,128)S(1)}, f32[6,1024]{1,0:T(8,128)}, u32[]{:S(2)}) copy-start(f32[6,1024]{1,0:T(8,128)} %wc_ref.1) | copy-start | bytes 73732
  3.0 0.7 %copy-start.3 = (s32[1024]{0:T(1024)S(1)}, s32[1024]{0:T(1024)}, u32[]{:S(2)}) copy-start(s32[1024]{0:T(1024)} %param.13) | copy-start | bytes 12292
  3.7 0.7 %copy-start.4 = (s32[1024]{0:T(1024)S(1)}, s32[1024]{0:T(1024)}, u32[]{:S(2)}) copy-start(s32[1024]{0:T(1024)} %param.14) | copy-start | bytes 12292
  4.4 8.0 %copy-start.8 = (f32[384]{0:T(512)S(1)}, f32[384]{0:T(512)}, u32[]{:S(2)}) copy-start(f32[384]{0:T(512)} %param.17) | copy-start | bytes 4612
  4.4 8.1 %collective-permute-start = (f32[32,1024]{1,0:T(8,128)S(1)}, f32[32,1024]{1,0:T(8,128)S(1)}, u32[]{:S(2)}, u32[]{:S(2)}) collective-permute-start(f32[32,1024]{1,0:T(8,128)S(1)} %pack_block.1.data_ref), channel_id=1, source_target_pairs={{0,2},{1,3},{2,0},{3,1},{4,6},{5,7},{6,4},{7,5}} | collective-permute-start | bytes 393224 | tf_op jit(solution)/shard_map/ppermute | solution.py:304
  12.5 6.5 %copy-start.5 = (f32[2,8,384,96]{2,3,1,0:T(8,128)S(1)}, f32[2,8,384,96]{2,3,1,0:T(8,128)}, u32[]{:S(2)}) copy-start(f32[2,8,384,96]{2,3,1,0:T(8,128)} %param.16) | copy-start | bytes 7077892
  12.5 6.5 %copy-start.6 = (bf16[2,2,384,384]{3,2,1,0:T(8,128)(2,1)S(1)}, bf16[2,2,384,384]{3,2,1,0:T(8,128)(2,1)}, u32[]{:S(2)}) copy-start(bf16[2,2,384,384]{3,2,1,0:T(8,128)(2,1)} %constant.5.clone.tab2_v) | copy-start | bytes 3538948
  12.6 6.5 %copy-start.7 = (bf16[2,384,768]{2,1,0:T(8,128)(2,1)S(1)}, bf16[2,384,768]{2,1,0:T(8,128)(2,1)}, u32[]{:S(2)}) copy-start(bf16[2,384,768]{2,1,0:T(8,128)(2,1)} %constant.4.clone.tab_ref) | copy-start | bytes 3538948
